TPU v7x, 32 devices: a whole 2x2x4 slice. The times are simulated.
32 devices in a mesh: facet: 8 (over y, x, core), sub: 4 (over z).
Axes of the slice: x: 2, y: 2, z: 4, core: 2. Of those that a mesh axis runs over, the one named last changes fastest.
Arguments:
- model_image: float32 [8, 128, 8192], P('facet'), may hold values from -6 to 6
- step_sizes: float32 [2], replicated, may hold values from 0.3 to 1
- facet_offsets: int32 [2, 8], replicated, may hold values from 0 to 57344
- col_offsets: int32 [4], P('sub'), may hold values from 0 to 65280
- row_offsets: int32 [4, 8], P('sub'), may hold values from 0 to 65280
- counts: int32 [4, 8], P('sub'), may hold values from 1024 to 4096, as said below
- vis_uv: int32 [2, 4, 8, 4096], P(None, 'sub', 'facet'), may hold values from 32 to 2015
- vis_obs: bfloat16 [2, 4, 8, 4096], P(None, 'sub', 'facet'), may hold values from -6 to 6
- vis_weight: bfloat16 [4, 8, 4096], P('sub', 'facet'), may hold values from 0.25 to 4
Outputs:
- updated_image: float32 [8, 128, 8192], P('facet')
- residual_vis: float32 [2, 4, 8, 4096], P(None, 'sub', 'facet')
Inputs may be any that keep to these rules, and one draw needn't show every extreme that they name: The visibilities of a subgrid fill its first counts slots; every draw has a subgrid with exactly 4096 visibilities and one with exactly 1024.
All inputs are finite; a program needn't handle non-finite values.
Results may differ from a plain program's by a relative error of at most 0.017.
Values may be sent and summed in bfloat16 or wider, within the bound.
A program may use at most 64 MiB of HBM per device.

v0:
```python
import math
import jax
import jax.numpy as jnp
from jax import lax
from jax.sharding import PartitionSpec as P

NIMG = 65536
FW = 8192
FROWS = 128
SGW = 256
VCAP = 4096
VB = 512
OS = 8
KSUP = 4
ITERS = 2
two_pi = 2.0 * math.pi


def phase_index(frequency, pixels):
    pixel_low = pixels % 256
    pixel_high = pixels // 256
    return (frequency * pixel_low + frequency * pixel_high % (NIMG // 256) * 256) % NIMG


def row_table(frequency_start, pixel_start):
    frequency = frequency_start + jnp.arange(SGW, dtype=jnp.int32)
    pixels = pixel_start + jnp.arange(FROWS, dtype=jnp.int32)
    angles = phase_index(frequency[:, None], pixels[None, :]).astype(jnp.float32) * (two_pi / NIMG)
    return jnp.concatenate([jnp.cos(angles), jnp.sin(angles)], axis=1).astype(jnp.bfloat16)


def column_table(frequency_start, pixel_start):
    frequency = frequency_start + jnp.arange(SGW, dtype=jnp.int32)
    pixels = pixel_start + jnp.arange(FW, dtype=jnp.int32)
    angles = phase_index(frequency[None, :], pixels[:, None]).astype(jnp.float32) * (two_pi / NIMG)
    return jnp.concatenate([jnp.cos(angles), -jnp.sin(angles)], axis=1).astype(jnp.bfloat16)


def expand_section(section_rows):
    real_half = section_rows[:, :SGW]
    imag_half = section_rows[:, SGW:]
    lower_rows = jnp.concatenate([imag_half, -real_half], axis=1)
    return jnp.concatenate([section_rows, lower_rows], axis=0)


def fold_back(back_rows):
    real_part = back_rows[..., :FROWS, :SGW] - back_rows[..., FROWS:, SGW:]
    imag_part = back_rows[..., :FROWS, SGW:] + back_rows[..., FROWS:, :SGW]
    return jnp.concatenate([real_part, imag_part], axis=-1)


def kernel_rows(position):
    offset = (jnp.arange(SGW, dtype=jnp.int32) * OS + OS // 2)[None, :] - position[:, None]
    distance = offset.astype(jnp.float32) / OS
    inside = jnp.abs(offset) <= KSUP * OS
    return jnp.where(inside, jnp.exp(-0.5 * distance * distance), 0.0).astype(jnp.bfloat16)


def block_pass(grid_bf, row_positions, column_positions, observed, weight, is_live):
    row_kernel = kernel_rows(row_positions)
    column_kernel = kernel_rows(column_positions)
    sampled = jnp.dot(row_kernel, grid_bf, preferred_element_type=jnp.float32)
    column_float = column_kernel.astype(jnp.float32)
    predicted_real = jnp.sum(sampled[:, :SGW] * column_float, axis=1)
    predicted_imag = jnp.sum(sampled[:, SGW:] * column_float, axis=1)
    weight_float = weight.astype(jnp.float32)
    residual_real = jnp.where(
        is_live, weight_float * (observed[0].astype(jnp.float32) - predicted_real), 0.0
    )
    residual_imag = jnp.where(
        is_live, weight_float * (observed[1].astype(jnp.float32) - predicted_imag), 0.0
    )
    weighted = jnp.concatenate(
        [residual_real[:, None] * column_float, residual_imag[:, None] * column_float], axis=1
    ).astype(jnp.bfloat16)
    block_grid = lax.dot_general(
        row_kernel, weighted, (((0,), (0,)), ((), ())), preferred_element_type=jnp.float32
    )
    return (block_grid, jnp.stack([residual_real, residual_imag]))


def sweep_blocks(grid_bf, positions, observed, weight, live_total, blocks):
    length = positions.shape[1]

    def one_block(block_index, running):
        grid_sum, residual = running
        first_row = (block_index * VB).astype(jnp.int32)
        position_part = lax.dynamic_slice_in_dim(positions, first_row, VB, 1)
        observed_part = lax.dynamic_slice_in_dim(observed, first_row, VB, 1)
        weight_part = lax.dynamic_slice_in_dim(weight, first_row, VB, 0)
        is_live = first_row + jnp.arange(VB, dtype=jnp.int32) < live_total
        block_grid, values = block_pass(
            grid_bf, position_part[0], position_part[1], observed_part, weight_part, is_live
        )
        residual = lax.dynamic_update_slice(residual, values, (jnp.int32(0), first_row))
        return (grid_sum + block_grid, residual)

    starting = (jnp.zeros((SGW, 2 * SGW), jnp.float32), jnp.zeros((2, length), jnp.float32))
    return lax.fori_loop(0, blocks, one_block, starting)


def local(
    model_image,
    step_sizes,
    facet_offsets,
    col_offsets,
    row_offsets,
    counts,
    vis_uv,
    vis_obs,
    vis_weight,
):
    facet_count = lax.axis_size("facet")
    norm_factor = 1.0 / math.sqrt(facet_count * FROWS * FW)
    my_facet = lax.axis_index("facet")
    columns_factor = column_table(col_offsets[0], facet_offsets[1, my_facet])
    my_rows = row_offsets[0]
    column_rows = jax.vmap(lambda single: row_table(single, facet_offsets[0, my_facet]))(my_rows)
    facet_rows = jax.vmap(lambda offset: row_table(my_rows[my_facet], offset))(facet_offsets[0])
    own_count = counts[0, my_facet]
    positions = vis_uv[:, 0, 0]
    observed = vis_obs[:, 0, 0]
    weight = vis_weight[0, 0]
    model_now = model_image[0]
    residual = jnp.zeros((2, VCAP), jnp.float32)
    for cycle_index in range(ITERS):
        section_rows = jnp.dot(
            model_now.astype(jnp.bfloat16), columns_factor, preferred_element_type=jnp.float32
        ).astype(jnp.bfloat16)
        pieces = lax.all_gather(section_rows[None], "facet", axis=0, tiled=True)
        expanded_pieces = jax.vmap(expand_section)(pieces)
        summed = lax.dot_general(
            facet_rows,
            expanded_pieces,
            (((0, 2), (0, 1)), ((), ())),
            preferred_element_type=jnp.float32,
        )
        grid_bf = (norm_factor * summed).astype(jnp.bfloat16)
        gridded, residual = sweep_blocks(
            grid_bf, positions, observed, weight, own_count, (own_count + VB - 1) // VB
        )
        gridded_bf = gridded.astype(jnp.bfloat16)
        add_pieces = lax.all_gather(gridded_bf[None], "facet", axis=0, tiled=True)
        add_number = add_pieces.shape[0]
        back_rows = lax.dot_general(
            column_rows.reshape(add_number * SGW, 2 * FROWS),
            add_pieces.reshape(add_number * SGW, 2 * SGW),
            (((0,), (0,)), ((), ())),
            preferred_element_type=jnp.float32,
        )
        adjoint_rows = fold_back(back_rows).astype(jnp.bfloat16)
        partial_gradient = lax.dot_general(
            adjoint_rows,
            columns_factor,
            (((1,), (1,)), ((), ())),
            preferred_element_type=jnp.float32,
        )
        gradient = lax.psum(partial_gradient.astype(jnp.bfloat16), "sub").astype(jnp.float32)
        model_now = model_now + step_sizes[cycle_index] * (norm_factor * gradient)
    return (model_now[None], residual.reshape(2, 1, 1, VCAP))


def solution(mesh):
    in_specs = (
        P("facet", None, None),
        P(),
        P(),
        P("sub"),
        P("sub", None),
        P("sub", None),
        P(None, "sub", "facet", None),
        P(None, "sub", "facet", None),
        P("sub", "facet", None),
    )
    out_specs = (P("facet", None, None), P(None, "sub", "facet", None))
    return jax.shard_map(local, mesh=mesh, in_specs=in_specs, out_specs=out_specs, check_vma=False)
```

profile of v0, /device:TPU:0, one launch (start us, length us, event | category | flops | bytes accessed | tf_op | source)
XLA Modules:
  0.0 421.7 jit_solution(10102998328427896458)
XLA Ops:
  7.2 1.4 constant_dynamic-slice_fusion.4
  8.7 0.7 add_select_fusion.6
  10.0 42.6 %cosine_convert_fusion = (bf16[8192,256]{1,0:T(8,128)(2,1)S(1)}, bf16[8192,256]{1,0:T(8,128)(2,1)S(1)}) fusion(s32[8192]{0:T(1024)S(1)} %get-tuple-element.372, s32[8192]{0:T(1024)S(1)} %get-tuple-element.373, s32[256]{0:T(256)S(1)} %iota_add_fusion.3), kind=kLoop, calls=%fused_computation.117 | loop fusion | flops 65011712 | bytes 8455168 | tf_op jit(solution)/shard_map/convert.12
  52.6 1.9 copy-done.2
  54.5 1.4 copy-done.5
  56.0 3.1 fusion.115
  59.1 0.6 constant_dynamic-slice_fusion.3
  60.4 0.6 constant_dynamic-slice_fusion.2
  61.1 0.6 iota_add_fusion.4
  61.9 5.0 %cosine_convert_fusion.1 = (bf16[8,256,128]{2,1,0:T(8,128)(2,1)S(1)}, bf16[8,256,128]{2,1,0:T(8,128)(2,1)S(1)}) fusion(s32[8,128]{1,0:T(8,128)S(1)} %get-tuple-element.369, s32[8,128]{1,0:T(8,128)S(1)} %get-tuple-element.368, s32[256]{0:T(256)S(1)} %iota_add_fusion.4), kind=kLoop, calls=%fused_computation.179 | loop fusion | flops 7864320 | bytes 1057792 | tf_op jit(solution)/shard_map/convert.14
  66.8 18.6 %all-gather.9.cloned.1.call-done = bf16[1024,512]{0,1:T(8,128)(2,1)} async-done(((bf16[128,512]{0,1:T(8,128)(2,1)}), bf16[1024,512]{0,1:T(8,128)(2,1)}) %all-gather.9.cloned.1.call-update) | async-done | bytes 1048592 | tf_op jit(solution)/shard_map/all_gather | solution.py:130
  85.4 1.5 copy.18
  87.0 0.7 fusion.108
  87.8 7.8 %while.30 = (s32[]{:T(128)}, f32[256,512]{1,0:T(8,128)S(1)}, s32[]{:T(128)}, s32[2,4096]{1,0:T(2,128)S(1)}, s32[]{:T(128)}, /*index=5*/bf16[4096]{0:T(1024)(128)...) while((s32[]{:T(128)}, f32[256,512]{1,0:T(8,128)S(1)}, ...), condition=%wide.region_3.4_spmd, body=%wide.region_0.3_spmd.sunk | while | flops 275649536 | bytes 4505811 | solution.py:99
  87.9 0.5 fusion.191
  88.9 0.7 fusion.193
  89.9 0.4 convolution_add_fusion.4
  90.5 0.5 fusion.191
  91.5 0.7 fusion.193
  92.5 0.4 convolution_add_fusion.4
  93.1 0.5 fusion.191
  94.1 0.7 fusion.193
  95.6 0.7 convert_element_type.203
  96.6 0.7 and_select_fusion
  97.3 5.0 %cosine_convert_fusion.2 = (bf16[8,256,128]{2,1,0:T(8,128)(2,1)S(1)}, bf16[8,256,128]{2,1,0:T(8,128)(2,1)S(1)}) fusion(s32[128]{0:T(128)S(1)} %get-tuple-element.370, s32[128]{0:T(128)S(1)} %get-tuple-element.371, s32[8,256]{1,0:T(8,128)S(1)} %iota_add_fusion.1), kind=kLoop, calls=%fused_computation.181 | loop fusion | flops 7864320 | bytes 1057792 | tf_op jit(solution)/shard_map/convert.16
  102.3 33.9 %all-gather.11.cloned.1.call-done = bf16[2048,512]{1,0:T(8,128)(2,1)} async-done(((bf16[256,512]{1,0:T(8,128)(2,1)}), bf16[2048,512]{1,0:T(8,128)(2,1)}) %all-gather.11.cloned.1.call-update) | async-done | bytes 2097168 | tf_op jit(solution)/shard_map/all_gather | solution.py:143
  136.2 2.5 convolution_bitcast_fusion.1
  139.1 6.4 %convolution_convert_fusion.1 = bf16[128,8192]{1,0:T(8,128)(2,1)} fusion(bf16[128,256]{1,0:T(8,128)(2,1)S(1)} %get-tuple-element.357, bf16[128,256]{1,0:T(8,128)(2,1)S(1)} %get-tuple-element.356, bf16[8192,256]{1,0:T(8,128)(2,1)} %copy-done.5, bf16[8192,256]{1,0:T(8,128)(2,1)S(1)} %copy-done.3), kind=kOutput, calls=%fused_computation.108 | convolution fusion | flops 1091829760 | bytes 10616832 | tf_op jit(solution)/shard_map/dot_general | solution.py:152
  145.6 0.6 fusion.159
  146.8 85.0 %all-reduce.3.cloned.1.call-done = bf16[128,8192]{1,0:T(8,128)(2,1)} async-done(((bf16[128,8192]{1,0:T(8,128)(2,1)}), bf16[128,8192]{1,0:T(8,128)(2,1)}) %all-reduce.3.cloned.1.call-update) | async-done | bytes 2097168 | tf_op jit(solution)/shard_map/psum | solution.py:158
  231.8 7.1 %fusion.111 = bf16[128,512]{1,0:T(8,128)(2,1)} fusion(bf16[128,8192]{1,0:T(8,128)(2,1)} %all-reduce.3.cloned.1.call-done, f32[1,128,8192]{2,1,0:T(8,128)} %param.13, f32[]{:T(128)} %bitcast.23, bf16[8192,256]{1,0:T(8,128)(2,1)} %copy-done.5, bf16[8192,256]{1,0:T(8,128)(2,1)} %copy-done.2), kind=kOutput, calls=%fused_computation.161 | convolution fusion | flops 1094778880 | bytes 14811140 | tf_op jit(solution)/shard_map/dot_general | solution.py:127
  239.0 22.5 %all-gather.13.cloned.1.call-done = bf16[1024,512]{1,0:T(8,128)(2,1)} async-done(((bf16[128,512]{1,0:T(8,128)(2,1)}), bf16[1024,512]{1,0:T(8,128)(2,1)}) %all-gather.13.cloned.1.call-update) | async-done | bytes 1048592 | tf_op jit(solution)/shard_map/all_gather | solution.py:130
  261.5 1.3 fusion.157
  262.8 1.9 fusion.105
  264.8 7.8 %while.31 = (s32[]{:T(128)}, f32[256,512]{1,0:T(8,128)S(1)}, f32[2,4096]{1,0:T(2,128)S(1)}, s32[]{:T(128)}, s32[2,4096]{1,0:T(2,128)S(1)}, /*index=5*/s32[]{:T(1...) while((s32[]{:T(128)}, f32[256,512]{1,0:T(8,128)S(1)}, ...), condition=%wide.region_8.9_spmd, body=%wide.region_5.8_spmd.sunk | while | flops 275650560 | bytes 4514015 | solution.py:99
  264.9 0.5 fusion.200
  265.9 0.7 fusion.202
  267.5 0.5 fusion.200
  268.5 0.7 fusion.202
  270.1 0.5 fusion.200
  271.1 0.7 fusion.202
  272.6 0.7 convert_element_type.209
  273.5 39.9 %all-gather.15.cloned.1.call-done = bf16[2048,512]{1,0:T(8,128)(2,1)} async-done(((bf16[256,512]{1,0:T(8,128)(2,1)}), bf16[2048,512]{1,0:T(8,128)(2,1)}) %all-gather.15.cloned.1.call-update) | async-done | bytes 2097168 | tf_op jit(solution)/shard_map/all_gather | solution.py:143
  313.4 2.5 convolution_bitcast_fusion
  316.2 6.5 %convolution_convert_fusion = bf16[128,8192]{1,0:T(8,128)(2,1)} fusion(bf16[128,256]{1,0:T(8,128)(2,1)S(1)} %get-tuple-element.355, bf16[128,256]{1,0:T(8,128)(2,1)S(1)} %get-tuple-element.354, bf16[8192,256]{1,0:T(8,128)(2,1)} %copy-done.5, bf16[8192,256]{1,0:T(8,128)(2,1)S(1)} %copy-done.4), kind=kOutput, calls=%fused_computation.107 | convolution fusion | flops 1091829760 | bytes 10616832 | tf_op jit(solution)/shard_map/dot_general | solution.py:152
  323.3 0.6 reshape.276
  324.0 85.1 %all-reduce.5.cloned.1.call-done = bf16[128,8192]{1,0:T(8,128)(2,1)} async-done(((bf16[128,8192]{1,0:T(8,128)(2,1)}), bf16[128,8192]{1,0:T(8,128)(2,1)}) %all-reduce.5.cloned.1.call-update) | async-done | bytes 2097168 | tf_op jit(solution)/shard_map/psum | solution.py:158
  409.0 5.8 %add_bitcast_fusion = f32[1,128,8192]{2,1,0:T(8,128)} fusion(bf16[128,8192]{1,0:T(8,128)(2,1)} %all-reduce.5.cloned.1.call-done, bf16[128,8192]{1,0:T(8,128)(2,1)S(1)} %copy-done.6, f32[1,128,8192]{2,1,0:T(8,128)} %param.13, f32[]{:T(128)} %bitcast.28, f32[]{:T(128)} %bitcast.23), kind=kLoop, calls=%fused_computation.120 | loop fusion | flops 6291456 | bytes 12582920 | tf_op jit(solution)/shard_map/broadcast_in_dim | solution.py:160
  (85 shorter events, 8.5 us)
Async XLA Ops:
  7.2 52.0 %copy-start = (s32[1,8]{1,0:T(1,128)S(1)}, s32[1,8]{1,0:T(1,128)}, u32[]{:S(2)}) copy-start(s32[1,8]{1,0:T(1,128)} %param.18) | copy-start | bytes 100
  7.2 78.2 %all-gather.9.cloned.1.call-start = ((), (), s32[]{:S(2)}) async-start(), calls=%async_computation.2 | async-start | bytes 1179648 | tf_op jit(solution)/shard_map/all_gather | solution.py:130
  10.0 46.0 %copy-start.1 = (f32[1,128,8192]{2,1,0:T(8,128)S(1)}, f32[1,128,8192]{2,1,0:T(8,128)}, u32[]{:S(2)}) copy-start(f32[1,128,8192]{2,1,0:T(8,128)} %param.13) | copy-start | bytes 12582916
  52.6 2.0 copy-start.2
  52.6 3.4 copy-start.5
  56.0 4.4 %copy-start.12 = (s32[1,8]{1,0:T(1,128)S(1)}, s32[1,8]{1,0:T(1,128)}, u32[]{:S(2)}) copy-start(s32[1,8]{1,0:T(1,128)} %param.17) | copy-start | bytes 100
  56.0 5.0 %copy-start.8 = (s32[2,1,1,4096]{3,2,1,0:T(1,128)S(1)}, s32[2,1,1,4096]{3,2,1,0:T(1,128)}, u32[]{:S(2)}) copy-start(s32[2,1,1,4096]{3,2,1,0:T(1,128)} %param.19) | copy-start | bytes 98308
  56.0 5.1 %copy-start.9 = (bf16[1,1,4096]{2,1,0:T(2,128)(2,1)S(1)}, bf16[1,1,4096]{2,1,0:T(2,128)(2,1)}, u32[]{:S(2)}) copy-start(bf16[1,1,4096]{2,1,0:T(2,128)(2,1)} %param.21) | copy-start | bytes 24580
  56.0 5.8 %copy-start.11 = (s32[2,8]{1,0:T(2,128)S(1)}, s32[2,8]{1,0:T(2,128)}, u32[]{:S(2)}) copy-start(s32[2,8]{1,0:T(2,128)} %param.15) | copy-start | bytes 196
  59.1 77.2 %all-gather.11.cloned.1.call-start = ((), (), s32[]{:S(2)}) async-start(), calls=%async_computation.3 | async-start | bytes 2359296 | tf_op jit(solution)/shard_map/all_gather | solution.py:143
  87.0 0.8 copy-start.7
  96.3 135.5 %all-reduce.3.cloned.1.call-start = ((), (), s32[]{:S(2)}) async-start(), calls=%async_computation | async-start | bytes 4194304 | tf_op jit(solution)/shard_map/psum | solution.py:158
  136.2 2.8 copy-start.3
  139.1 6.5 %copy-start.10 = (f32[2]{0:T(128)S(1)}, f32[2]{0:T(128)}, u32[]{:S(2)}) copy-start(f32[2]{0:T(128)} %param.14) | copy-start | bytes 28
  145.5 116.0 %all-gather.13.cloned.1.call-start = ((), (), s32[]{:S(2)}) async-start(), calls=%async_computation.4 | async-start | bytes 1179648 | tf_op jit(solution)/shard_map/all_gather | solution.py:130
  239.0 74.4 %all-gather.15.cloned.1.call-start = ((), (), s32[]{:S(2)}) async-start(), calls=%async_computation.5 | async-start | bytes 2359296 | tf_op jit(solution)/shard_map/all_gather | solution.py:143
  273.4 135.6 %all-reduce.5.cloned.1.call-start = ((), (), s32[]{:S(2)}) async-start(), calls=%async_computation.1 | async-start | bytes 4194304 | tf_op jit(solution)/shard_map/psum | solution.py:158
  313.4 2.8 copy-start.4
  316.2 92.8 %copy-start.6 = (bf16[128,8192]{1,0:T(8,128)(2,1)S(1)}, bf16[128,8192]{1,0:T(8,128)(2,1)}, u32[]{:S(2)}) copy-start(bf16[128,8192]{1,0:T(8,128)(2,1)} %all-reduce.3.cloned.1.call-done) | copy-start | bytes 6291460
Sparse Core Ops, SparseCore 0:
  59.2 26.1 all-gather.8
  96.5 39.7 all-gather.10
  145.6 86.1 all-reduce.2
  239.1 22.3 all-gather.12
  273.5 39.8 all-gather.14
  322.9 86.1 all-reduce.4
where the time goes:
time: 422 us
  waiting for transfers between devices  285 us (68%)
  other arithmetic  72.4 us (17%)
  matrix products  36.5 us (9%)
  between operations  16.9 us (4%)
  local copies, waits for them, and re-layouts  10 us (2%)
    psum x2, waiting for transfers between devices, local(): lax.psum(partial_gradient.astype(jnp.bfloat16), 'sub').astype(jnp.float32)  170 us
    all_gather x2, waiting for transfers between devices, local(): add_pieces = lax.all_gather(gridded_bf[None], 'facet', axis=0, tiled=True)  73.8 us
    another operation x11, other arithmetic  54.5 us
    all_gather x2, waiting for transfers between devices, local(): pieces = lax.all_gather(section_rows[None], 'facet', axis=0, tiled=True)  41.1 us
    dot_general x2, matrix products, local(): lax.dot_general(adjoint_rows, columns_factor, (((1,), (1,)), ((), ())), p...  12.9 us
    dot_general x2, matrix products, local(): jnp.dot(model_now.astype(jnp.bfloat16), columns_factor, preferred_element...  10.2 us
  transfers between devices with their start and end apart: 6, of which 6 were waited for; matrix products, arithmetic and copies ran while one was open for 3% of the time, Pallas kernels for 0%

commit v1 on v0

--- a/solution.py
+++ b/solution.py
@@ -155,7 +155,9 @@
             (((1,), (1,)), ((), ())),
             preferred_element_type=jnp.float32,
         )
-        gradient = lax.psum(partial_gradient.astype(jnp.bfloat16), "sub").astype(jnp.float32)
+        gradient = jnp.sum(
+            lax.all_gather(partial_gradient.astype(jnp.bfloat16), "sub"), axis=0
+        ).astype(jnp.float32)
         model_now = model_now + step_sizes[cycle_index] * (norm_factor * gradient)
     return (model_now[None], residual.reshape(2, 1, 1, VCAP))
 

time: 422 us -> 561 us (1.33)
  waiting for transfers between devices: 285 us -> 411 us
  other arithmetic: 72.4 us -> 84.8 us
    all_gather x0 -> x2, waiting for transfers between devices: none -> 297 us  [local(): lax.all_gather(partial_gradient.astype(jnp.bfloat16), 'sub')]
    psum x2 -> x0, waiting for transfers between devices: 170 us -> none  [local(): lax.psum(partial_gradient.astype(jnp.bfloat16), 'sub').astype(jnp.float32)]
    reduce_sum x0 -> x2, other arithmetic: none -> 12 us  [local(): jnp.sum(lax.all_gather(partial_gradient.astype(jnp.bfloat16), 'sub'), axi...]
    add x0 -> x1, other arithmetic: none -> 5.85 us  [local(): model_now = model_now + step_sizes[cycle_index] * (norm_factor * gradient)]
    broadcast_in_dim x1 -> x0, other arithmetic: 5.81 us -> none  [local(): return (model_now[None], residual.reshape(2, 1, 1, VCAP))]
where the time goes in v1:
time: 561 us; the launch traced here: 560 us
  waiting for transfers between devices  411 us (73%)
  other arithmetic  84.8 us (15%)
  matrix products  36.1 us (6%)
  between operations  17.1 us (3%)
  local copies, waits for them, and re-layouts  10.2 us (2%)
    all_gather x2, waiting for transfers between devices, local(): lax.all_gather(partial_gradient.astype(jnp.bfloat16), 'sub')  297 us
    all_gather x2, waiting for transfers between devices, local(): add_pieces = lax.all_gather(gridded_bf[None], 'facet', axis=0, tiled=True)  74.2 us
    another operation x11, other arithmetic  54.5 us
    all_gather x2, waiting for transfers between devices, local(): pieces = lax.all_gather(section_rows[None], 'facet', axis=0, tiled=True)  40.1 us
    dot_general x2, matrix products, local(): lax.dot_general(adjoint_rows, columns_factor, (((1,), (1,)), ((), ())), p...  12.7 us
    reduce_sum x2, other arithmetic, local(): jnp.sum(lax.all_gather(partial_gradient.astype(jnp.bfloat16), 'sub'), axi...  12 us
  transfers between devices with their start and end apart: 6, of which 6 were waited for; matrix products, arithmetic and copies ran while one was open for 3% of the time, Pallas kernels for 0%

profile of v1, /device:TPU:0, one launch (start us, length us, event | category | flops | bytes accessed | tf_op | source)
XLA Modules:
  0.0 560.4 jit_solution(10066084918278083342)
XLA Ops:
  7.2 1.4 constant_dynamic-slice_fusion.4
  8.6 0.7 add_select_fusion.6
  10.0 42.6 %cosine_convert_fusion = (bf16[8192,256]{1,0:T(8,128)(2,1)S(1)}, bf16[8192,256]{1,0:T(8,128)(2,1)S(1)}) fusion(s32[8192]{0:T(1024)S(1)} %get-tuple-element.372, s32[8192]{0:T(1024)S(1)} %get-tuple-element.373, s32[256]{0:T(256)S(1)} %iota_add_fusion.3), kind=kLoop, calls=%fused_computation.117 | loop fusion | flops 65011712 | bytes 8455168 | tf_op jit(solution)/shard_map/convert.14
  52.6 2.0 copy-done.2
  54.6 1.4 copy-done.5
  56.0 3.0 fusion.115
  59.1 0.7 constant_dynamic-slice_fusion.3
  60.5 0.6 constant_dynamic-slice_fusion.2
  61.2 0.6 iota_add_fusion.4
  62.0 5.0 cosine_convert_fusion.1
  66.9 18.5 %all-gather.13.cloned.1.call-done = bf16[1024,512]{0,1:T(8,128)(2,1)} async-done(((bf16[128,512]{0,1:T(8,128)(2,1)}), bf16[1024,512]{0,1:T(8,128)(2,1)}) %all-gather.13.cloned.1.call-update) | async-done | bytes 1048592 | tf_op jit(solution)/shard_map/all_gather | solution.py:130
  85.4 1.5 copy.18
  87.0 0.7 fusion.108
  87.8 7.9 %while.30 = (s32[]{:T(128)}, f32[256,512]{1,0:T(8,128)S(1)}, s32[]{:T(128)}, s32[2,4096]{1,0:T(2,128)S(1)}, s32[]{:T(128)}, /*index=5*/bf16[4096]{0:T(1024)(128)...) while((s32[]{:T(128)}, f32[256,512]{1,0:T(8,128)S(1)}, ...), condition=%wide.region_3.4_spmd, body=%wide.region_0.3_spmd.sunk | while | flops 275649536 | bytes 4505811 | solution.py:99
  87.9 0.5 fusion.191
  88.9 0.8 fusion.193
  90.5 0.5 fusion.191
  91.5 0.8 fusion.193
  93.2 0.5 fusion.191
  94.2 0.8 fusion.193
  95.7 0.8 convert_element_type.223
  96.7 0.7 and_select_fusion
  97.5 5.0 cosine_convert_fusion.2
  102.5 34.2 %all-gather.15.cloned.1.call-done = bf16[2048,512]{1,0:T(8,128)(2,1)} async-done(((bf16[256,512]{1,0:T(8,128)(2,1)}), bf16[2048,512]{1,0:T(8,128)(2,1)}) %all-gather.15.cloned.1.call-update) | async-done | bytes 2097168 | tf_op jit(solution)/shard_map/all_gather | solution.py:143
  136.7 2.5 convolution_bitcast_fusion.1
  139.5 6.3 %convolution_convert_fusion.1 = bf16[128,8192]{1,0:T(8,128)(2,1)} fusion(bf16[128,256]{1,0:T(8,128)(2,1)S(1)} %get-tuple-element.357, bf16[128,256]{1,0:T(8,128)(2,1)S(1)} %get-tuple-element.356, bf16[8192,256]{1,0:T(8,128)(2,1)} %copy-done.5, bf16[8192,256]{1,0:T(8,128)(2,1)S(1)} %copy-done.3), kind=kOutput, calls=%fused_computation.108 | convolution fusion | flops 1091829760 | bytes 10616832 | tf_op jit(solution)/shard_map/dot_general | solution.py:152
  145.9 0.6 fusion.159
  147.2 148.4 %all-gather.17.cloned.1.call-done = bf16[512,8192]{1,0:T(8,128)(2,1)} async-done(((bf16[128,8192]{1,0:T(8,128)(2,1)}), bf16[512,8192]{1,0:T(8,128)(2,1)}) %all-gather.17.cloned.1.call-update) | async-done | bytes 8388624 | tf_op jit(solution)/shard_map/all_gather | solution.py:159
  295.6 5.1 reduce_sum.78
  300.8 6.8 %fusion.111 = bf16[128,512]{1,0:T(8,128)(2,1)} fusion(f32[1,128,8192]{2,1,0:T(8,128)} %param.13, bf16[128,8192]{1,0:T(8,128)(2,1)S(1)} %reduce_sum.78, f32[]{:T(128)} %bitcast.24, bf16[8192,256]{1,0:T(8,128)(2,1)} %copy-done.5, bf16[8192,256]{1,0:T(8,128)(2,1)} %copy-done.2), kind=kOutput, calls=%fused_computation.163 | convolution fusion | flops 1094778880 | bytes 14811140 | tf_op jit(solution)/shard_map/dot_general | solution.py:127
  307.6 21.7 %all-gather.19.cloned.1.call-done = bf16[1024,512]{1,0:T(8,128)(2,1)} async-done(((bf16[128,512]{1,0:T(8,128)(2,1)}), bf16[1024,512]{1,0:T(8,128)(2,1)}) %all-gather.19.cloned.1.call-update) | async-done | bytes 1048592 | tf_op jit(solution)/shard_map/all_gather | solution.py:130
  329.3 1.3 fusion.157
  330.5 1.9 fusion.105
  332.6 8.0 %while.31 = (s32[]{:T(128)}, f32[256,512]{1,0:T(8,128)S(1)}, f32[2,4096]{1,0:T(2,128)S(1)}, s32[]{:T(128)}, s32[2,4096]{1,0:T(2,128)S(1)}, /*index=5*/s32[]{:T(1...) while((s32[]{:T(128)}, f32[256,512]{1,0:T(8,128)S(1)}, ...), condition=%wide.region_8.9_spmd, body=%wide.region_5.8_spmd.sunk | while | flops 275650560 | bytes 4514015 | solution.py:99
  332.7 0.5 fusion.200
  333.7 0.8 fusion.202
  335.3 0.5 fusion.200
  336.3 0.8 fusion.202
  338.0 0.5 fusion.200
  339.0 0.8 fusion.202
  340.6 0.8 convert_element_type.229
  341.6 40.0 %all-gather.21.cloned.1.call-done = bf16[2048,512]{1,0:T(8,128)(2,1)} async-done(((bf16[256,512]{1,0:T(8,128)(2,1)}), bf16[2048,512]{1,0:T(8,128)(2,1)}) %all-gather.21.cloned.1.call-update) | async-done | bytes 2097168 | tf_op jit(solution)/shard_map/all_gather | solution.py:143
  381.6 2.6 convolution_bitcast_fusion
  384.6 6.4 %convolution_convert_fusion = bf16[128,8192]{1,0:T(8,128)(2,1)} fusion(bf16[128,256]{1,0:T(8,128)(2,1)S(1)} %get-tuple-element.355, bf16[128,256]{1,0:T(8,128)(2,1)S(1)} %get-tuple-element.354, bf16[8192,256]{1,0:T(8,128)(2,1)} %copy-done.5, bf16[8192,256]{1,0:T(8,128)(2,1)S(1)} %copy-done.4), kind=kOutput, calls=%fused_computation.107 | convolution fusion | flops 1091829760 | bytes 10616832 | tf_op jit(solution)/shard_map/dot_general | solution.py:152
  391.7 0.6 reshape.302
  392.3 148.5 %all-gather.23.cloned.1.call-done = bf16[512,8192]{1,0:T(8,128)(2,1)} async-done(((bf16[128,8192]{1,0:T(8,128)(2,1)}), bf16[512,8192]{1,0:T(8,128)(2,1)}) %all-gather.23.cloned.1.call-update) | async-done | bytes 8388624 | tf_op jit(solution)/shard_map/all_gather | solution.py:159
  540.8 6.9 %reduce_sum.79 = bf16[128,8192]{1,0:T(8,128)(2,1)} reduce(bf16[4,128,8192]{2,1,0:T(8,128)(2,1)} %bitcast.105, bf16[]{:T(256)} %constant.289.clone.1), dimensions={0}, to_apply=%region_9.10 | reduce | flops 3145728 | bytes 10485762 | tf_op jit(solution)/shard_map/reduce_sum | solution.py:158
  547.7 5.9 %bitcast_add_fusion = f32[1,128,8192]{2,1,0:T(8,128)} fusion(f32[1,128,8192]{2,1,0:T(8,128)} %param.13, bf16[128,8192]{1,0:T(8,128)(2,1)} %reduce_sum.79, bf16[128,8192]{1,0:T(8,128)(2,1)S(1)} %reduce_sum.78, f32[]{:T(128)} %bitcast.31, f32[]{:T(128)} %bitcast.24), kind=kLoop, calls=%fused_computation.118 | loop fusion | flops 6291456 | bytes 12582920 | tf_op jit(solution)/shard_map/add | solution.py:161
  (91 shorter events, 9.6 us)
Async XLA Ops:
  7.2 51.9 %copy-start = (s32[1,8]{1,0:T(1,128)S(1)}, s32[1,8]{1,0:T(1,128)}, u32[]{:S(2)}) copy-start(s32[1,8]{1,0:T(1,128)} %param.18) | copy-start | bytes 100
  7.2 78.2 %all-gather.13.cloned.1.call-start = ((), (), s32[]{:S(2)}) async-start(), calls=%async_computation | async-start | bytes 1179648 | tf_op jit(solution)/shard_map/all_gather | solution.py:130
  10.0 46.0 %copy-start.1 = (f32[1,128,8192]{2,1,0:T(8,128)S(1)}, f32[1,128,8192]{2,1,0:T(8,128)}, u32[]{:S(2)}) copy-start(f32[1,128,8192]{2,1,0:T(8,128)} %param.13) | copy-start | bytes 12582916
  52.6 2.0 copy-start.2
  52.6 3.4 copy-start.5
  56.0 4.5 copy-start.14
  56.0 5.2 copy-start.10
  56.0 5.2 copy-start.11
  56.0 5.9 %copy-start.13 = (s32[2,8]{1,0:T(2,128)S(1)}, s32[2,8]{1,0:T(2,128)}, u32[]{:S(2)}) copy-start(s32[2,8]{1,0:T(2,128)} %param.15) | copy-start | bytes 196
  59.0 77.6 %all-gather.15.cloned.1.call-start = ((), (), s32[]{:S(2)}) async-start(), calls=%async_computation.1 | async-start | bytes 2359296 | tf_op jit(solution)/shard_map/all_gather | solution.py:143
  87.0 0.8 copy-start.9
  96.5 199.1 %all-gather.17.cloned.1.call-start = ((), (), s32[]{:S(2)}) async-start(), calls=%async_computation.2 | async-start | bytes 10485760 | tf_op jit(solution)/shard_map/all_gather | solution.py:159
  102.5 43.4 %copy-start.6 = (bf16[8,256,128]{2,1,0:T(8,128)(2,1)}, bf16[8,256,128]{2,1,0:T(8,128)(2,1)S(1)}, u32[]{:S(2)}) copy-start(bf16[8,256,128]{2,1,0:T(8,128)(2,1)S(1)} %get-tuple-element.360) | copy-start | bytes 1572868
  102.5 43.3 %copy-start.8 = (bf16[8,256,128]{2,1,0:T(8,128)(2,1)}, bf16[8,256,128]{2,1,0:T(8,128)(2,1)S(1)}, u32[]{:S(2)}) copy-start(bf16[8,256,128]{2,1,0:T(8,128)(2,1)S(1)} %get-tuple-element.361) | copy-start | bytes 1572868
  136.7 2.8 copy-start.3
  139.5 6.4 %copy-start.12 = (f32[2]{0:T(128)S(1)}, f32[2]{0:T(128)}, u32[]{:S(2)}) copy-start(f32[2]{0:T(128)} %param.14) | copy-start | bytes 28
  145.9 183.4 %all-gather.19.cloned.1.call-start = ((), (), s32[]{:S(2)}) async-start(), calls=%async_computation.3 | async-start | bytes 1179648 | tf_op jit(solution)/shard_map/all_gather | solution.py:130
  307.6 74.0 %all-gather.21.cloned.1.call-start = ((), (), s32[]{:S(2)}) async-start(), calls=%async_computation.4 | async-start | bytes 2359296 | tf_op jit(solution)/shard_map/all_gather | solution.py:143
  332.6 49.1 %copy-start.7 = (bf16[8,256,128]{2,1,0:T(8,128)(2,1)S(1)}, bf16[8,256,128]{2,1,0:T(8,128)(2,1)}, u32[]{:S(2)}) copy-start(bf16[8,256,128]{2,1,0:T(8,128)(2,1)} %copy-done.6) | copy-start | bytes 1572868
  341.3 199.4 %all-gather.23.cloned.1.call-start = ((), (), s32[]{:S(2)}) async-start(), calls=%async_computation.5 | async-start | bytes 10485760 | tf_op jit(solution)/shard_map/all_gather | solution.py:159
  381.6 3.0 copy-start.4
Sparse Core Ops, SparseCore 0:
  59.2 26.1 all-gather.12
  96.6 40.0 all-gather.14
  146.0 149.6 all-gather.16
  307.7 21.5 all-gather.18
  341.5 40.1 all-gather.20
  391.1 149.5 all-gather.22
